TPU v7x, 32 devices: a whole 2x2x4 slice. The times are simulated.
32 devices in a mesh: ka: 2 (over x), band: 16 (over z, y, core).
Axes of the slice: x: 2, y: 2, z: 4, core: 2. Of those that a mesh axis runs over, the one named last changes fastest.
Arguments:
- psi_hat: float32 [2, 12, 2, 128, 128, 128], P('ka', None, None, 'band'), may hold values from -1.5 to 1.5
- occupations: int32 [2, 12], P('ka'), may hold values from 0 to 2
- weights: int32 [2], P('ka'), may hold values from 1 to 6
- density_in: float32 [128, 128, 128], P('band'), may hold values from -12 to 12
- dens_hist: float32 [8, 128, 128, 128], P(None, 'band'), may hold values from -3 to 3
- resid_hist: float32 [8, 128, 128, 128], P(None, 'band'), may hold values from -12 to 12
Outputs:
- out_density: float32 [128, 128, 128], P('band')
- mixed_density: float32 [128, 128, 128], P('band')
All inputs are finite; a program needn't handle non-finite values.
Results may differ from a plain program's by a relative error of at most 0.0003.
Values sent between devices are 32-bit elements; how exact they have to be, the bound alone decides.
A program may use at most 128 MiB of HBM per device.

v0:
```python
from functools import partial
import jax
import jax.numpy as jnp
from jax import lax
from jax.sharding import PartitionSpec as P

NG = 128
highest = lax.Precision.HIGHEST
beta_mix = 0.3
regular = 0.01


def dft_tables():
    indices = jnp.arange(NG, dtype=jnp.int32)
    product = indices[:, None] * indices[None, :] % NG
    angles = product.astype(jnp.float32) * jnp.float32(2.0 * 3.141592653589793 / NG)
    return (jnp.cos(angles), jnp.sin(angles))


def rotate(pattern, real_part, imag_part, cosine_table, sine_table):
    einsum = partial(jnp.einsum, precision=highest)
    out_real = einsum(pattern, real_part, cosine_table) - einsum(pattern, imag_part, sine_table)
    out_imag = einsum(pattern, real_part, sine_table) + einsum(pattern, imag_part, cosine_table)
    return (out_real, out_imag)


def history_gram(resid_hist):
    return jnp.einsum("hzxy,gzxy->hg", resid_hist, resid_hist, precision=highest)


def local_sums(residual_now, resid_hist):
    projections = jnp.einsum("hzxy,zxy->h", resid_hist, residual_now, precision=highest)[:, None]
    return jnp.concatenate([history_gram(resid_hist), projections], axis=1)


def finish_mix(density, base_density, dens_hist, resid_hist, summed):
    gram = summed[:, :-1]
    projections = summed[:, -1]
    system = gram + regular * jnp.diag(jnp.diag(gram))
    chol_factor = jnp.linalg.cholesky(system)
    mix_coefs = jax.scipy.linalg.cho_solve((chol_factor, True), projections)
    update = jnp.einsum(
        "h,hzxy->zxy", mix_coefs, dens_hist + beta_mix * resid_hist, precision=highest
    )
    return base_density + beta_mix * (density - base_density) - update


def shards(psi_hat, occupations, weights, density_in, dens_hist, resid_hist):
    cosine_table, sine_table = dft_tables()
    weight_total = lax.psum(jnp.sum(weights.astype(jnp.float32)), "ka")
    after_kz = rotate("bpqk,kz->bzpq", psi_hat[0, :, 0], psi_hat[0, :, 1], cosine_table, sine_table)
    after_ky = rotate("bzpq,qy->bzpy", after_kz[0], after_kz[1], cosine_table, sine_table)
    stacked = jnp.stack(after_ky, axis=1)
    received = lax.all_to_all(stacked, "band", split_axis=2, concat_axis=3, tiled=True)
    real_part, imag_part = rotate(
        "bzpy,px->bzxy", received[:, 0], received[:, 1], cosine_table, sine_table
    )
    power = (real_part * real_part + imag_part * imag_part) * jnp.float32(1.0 / NG**3)
    occ_float = occupations[0].astype(jnp.float32)
    pool_term = jnp.einsum("b,bzxy->zxy", occ_float, power, precision=highest)
    pool_term = pool_term * (weights[0].astype(jnp.float32) / weight_total)
    share = lax.psum_scatter(pool_term, "ka", scatter_dimension=1, tiled=True)
    share_width = share.shape[1]
    share_start = lax.axis_index("ka") * share_width
    base_density = lax.dynamic_slice_in_dim(density_in, share_start, share_width, 1)
    dens_part = lax.dynamic_slice_in_dim(dens_hist, share_start, share_width, 2)
    resid_part = lax.dynamic_slice_in_dim(resid_hist, share_start, share_width, 2)
    partial_terms = local_sums(share - base_density, resid_part)
    summed = lax.psum(partial_terms, ("ka", "band"))
    mixed_share = finish_mix(share, base_density, dens_part, resid_part, summed)
    density, mixed_density = (
        lax.all_gather(share, "ka", axis=1, tiled=True),
        lax.all_gather(mixed_share, "ka", axis=1, tiled=True),
    )
    return (density, mixed_density)


def solution(mesh):
    return jax.shard_map(
        shards,
        mesh=mesh,
        in_specs=(
            P("ka", None, None, "band", None, None),
            P("ka", None),
            P("ka"),
            P("band", None, None),
            P(None, "band", None, None),
            P(None, "band", None, None),
        ),
        out_specs=(P("band", None, None), P("band", None, None)),
        check_vma=False,
    )
```

profile of v0, /device:TPU:0, one launch (start us, length us, event | category | flops | bytes accessed | tf_op | source)
XLA Modules:
  0.0 529.3 jit_solution(17351105606221677500)
XLA Ops:
  7.2 8.3 %fusion.2 = f32[128,12,8,128]{3,0,2,1:T(8,128)S(1)} fusion(f32[1,12,2,8,128,128]{5,4,3,2,1,0:T(8,128)} %param.6), kind=kOutput, calls=%fused_computation.7 | convolution fusion | flops 2416148480 | bytes 12582912 | tf_op jit(solution)/shard_map/bpqk,kz->bzpq/dot_general | solution.py:23
  15.5 6.2 %fusion.6 = f32[128,12,8,128]{3,0,2,1:T(8,128)S(1)} fusion(f32[1,12,2,8,128,128]{5,4,3,2,1,0:T(8,128)S(1)} %copy-done.1), kind=kOutput, calls=%fused_computation.11 | convolution fusion | flops 2416148480 | bytes 12582912 | tf_op jit(solution)/shard_map/bpqk,kz->bzpq/dot_general | solution.py:23
  21.7 8.7 %fusion.4 = f32[128,12,8,128]{3,0,2,1:T(8,128)S(1)} fusion(f32[1,12,2,8,128,128]{5,4,3,2,1,0:T(8,128)} %param.6), kind=kOutput, calls=%fused_computation.9 | convolution fusion | flops 2416148480 | bytes 12582912 | tf_op jit(solution)/shard_map/bpqk,kz->bzpq/dot_general | solution.py:22
  30.3 8.1 %fusion.8 = f32[128,12,8,128]{3,0,2,1:T(8,128)S(1)} fusion(f32[1,12,2,8,128,128]{5,4,3,2,1,0:T(8,128)} %param.6), kind=kOutput, calls=%fused_computation.13 | convolution fusion | flops 2416148480 | bytes 12582912 | tf_op jit(solution)/shard_map/bpqk,kz->bzpq/dot_general | solution.py:22
  38.5 7.4 %fusion.10 = f32[12,128,8,128]{3,1,2,0:T(8,128)} fusion(f32[128,12,8,128]{3,0,2,1:T(8,128)S(1)} %fusion.6, f32[128,12,8,128]{3,0,2,1:T(8,128)S(1)} %fusion.2), kind=kOutput, calls=%fused_computation.15 | convolution fusion | flops 2417721344 | bytes 18874368 | tf_op jit(solution)/shard_map/bzpq,qy->bzpy/dot_general | solution.py:23
  45.8 7.7 %fusion.12 = f32[12,128,8,128]{3,1,2,0:T(8,128)} fusion(f32[128,12,8,128]{3,0,2,1:T(8,128)S(1)} %fusion.6, f32[128,12,8,128]{3,0,2,1:T(8,128)S(1)} %fusion.2), kind=kOutput, calls=%fused_computation.17 | convolution fusion | flops 2417721344 | bytes 18874368 | tf_op jit(solution)/shard_map/bzpq,qy->bzpy/dot_general | solution.py:22
  53.5 8.2 %add_bitcast_fusion = f32[12,1,128,8,128]{4,2,3,0,1:T(8,128)S(1)} fusion(f32[12,128,8,128]{3,1,2,0:T(8,128)} %fusion.10, f32[128,12,8,128]{3,0,2,1:T(8,128)S(1)} %fusion.8, f32[128,12,8,128]{3,0,2,1:T(8,128)S(1)} %fusion.4), kind=kOutput, calls=%fused_computation.24 | convolution fusion | flops 2419294208 | bytes 25165824 | tf_op jit(solution)/shard_map/bzpq,qy->bzpy/dot_general | solution.py:23
  61.7 7.7 %subtract_bitcast_fusion = f32[12,1,128,8,128]{4,2,3,0,1:T(8,128)} fusion(f32[12,128,8,128]{3,1,2,0:T(8,128)S(1)} %copy-done.2, f32[128,12,8,128]{3,0,2,1:T(8,128)S(1)} %fusion.8, f32[128,12,8,128]{3,0,2,1:T(8,128)S(1)} %fusion.4), kind=kOutput, calls=%fused_computation.25 | convolution fusion | flops 2419294208 | bytes 25165824 | tf_op jit(solution)/shard_map/bzpq,qy->bzpy/dot_general | solution.py:22
  69.4 9.0 %pad_maximum_fusion = f32[12,2,128,8,128]{4,2,3,0,1:T(8,128)} fusion(f32[12,1,128,8,128]{4,2,3,0,1:T(8,128)S(1)} %add_bitcast_fusion, f32[12,1,128,8,128]{4,2,3,0,1:T(8,128)} %subtract_bitcast_fusion), kind=kLoop, calls=%fused_computation.1 | loop fusion | flops 3145728 | bytes 25165824 | tf_op jit(solution)/shard_map/stack | solution.py:53
  78.4 16.3 %copy.60 = f32[12,2,128,8,128]{4,3,0,1,2:T(8,128)} copy(f32[12,2,128,8,128]{4,2,3,0,1:T(8,128)} %pad_maximum_fusion) | data formatting | bytes 25165824 | tf_op jit(solution)/shard_map/stack | solution.py:53
  94.8 7.5 %all-to-all-start = ((f32[12,2,128,8,128]{4,3,0,1,2:T(8,128)}), f32[12,2,128,8,128]{4,3,0,1,2:T(8,128)}, u32[]{:S(2)}, u32[]{:S(2)}) async-start(f32[12,2,128,8,128]{4,3,0,1,2:T(8,128)} %copy.60), calls=%async_computation | async-start | bytes 25165824 | tf_op jit(solution)/shard_map/all_to_all | solution.py:54
  102.9 6.1 %psum.14 = f32[]{:T(128)} all-reduce(f32[]{:T(128)} %bitcast.28), channel_id=1, replica_groups=mesh['ka'=2,'band'=16] {'ka'}, use_global_device_ids=true, to_apply=%region_0.1 | all-reduce | flops 1 | bytes 8 | tf_op jit(solution)/shard_map/psum | solution.py:50
  109.7 216.1 %all-to-all-done = f32[12,2,128,8,128]{4,3,0,1,2:T(8,128)} async-done(((f32[12,2,128,8,128]{4,3,0,1,2:T(8,128)}), f32[12,2,128,8,128]{4,3,0,1,2:T(8,128)}, u32[]{:S(2)}, u32[]{:S(2)}) %all-to-all-start) | async-done | bytes 12582944 | tf_op jit(solution)/shard_map/all_to_all | solution.py:54
  325.8 10.8 %copy.121 = f32[12,2,8,16,8,128]{5,4,3,2,1,0:T(8,128)} copy(f32[12,2,8,16,8,128]{5,4,0,1,2,3:T(8,128)} %bitcast.18) | data formatting | bytes 25165824 | tf_op jit(solution)/shard_map/all_to_all | solution.py:54
  336.7 10.2 %fusion.18 = f32[128,12,8,128]{3,0,2,1:T(8,128)} fusion(f32[12,2,8,128,128]{4,3,2,1,0:T(8,128)} %bitcast.136), kind=kOutput, calls=%fused_computation.26 | convolution fusion | flops 2416148480 | bytes 12582912 | tf_op jit(solution)/shard_map/bzpy,px->bzxy/dot_general | solution.py:23
  346.9 7.8 %fusion.19 = f32[128,12,8,128]{3,0,2,1:T(8,128)} fusion(f32[12,2,8,128,128]{4,3,2,1,0:T(8,128)S(1)} %bitcast.137), kind=kOutput, calls=%fused_computation.27 | convolution fusion | flops 2416148480 | bytes 12582912 | tf_op jit(solution)/shard_map/bzpy,px->bzxy/dot_general | solution.py:22
  354.7 7.8 %fusion.20 = f32[128,12,8,128]{3,0,2,1:T(8,128)} fusion(f32[12,2,8,128,128]{4,3,2,1,0:T(8,128)S(1)} %bitcast.138), kind=kOutput, calls=%fused_computation.28 | convolution fusion | flops 2416148480 | bytes 12582912 | tf_op jit(solution)/shard_map/bzpy,px->bzxy/dot_general | solution.py:23
  362.4 11.7 %multiply_bitcast_fusion = f32[12,8,128,128]{3,2,1,0:T(8,128)S(1)} fusion(f32[128,12,8,128]{3,0,2,1:T(8,128)} %fusion.18, f32[128,12,8,128]{3,0,2,1:T(8,128)} %fusion.20, f32[128,12,8,128]{3,0,2,1:T(8,128)} %fusion.19, f32[12,2,8,128,128]{4,3,2,1,0:T(8,128)S(1)} %bitcast.139), kind=kOutput, calls=%fused_computation.23 | convolution fusion | flops 2425585664 | bytes 31457280 | tf_op jit(solution)/shard_map/bzpy,px->bzxy/dot_general | solution.py:22
  374.1 10.8 %fusion = f32[1,8,128,128]{3,0,2,1:T(1,128)S(1)} fusion(f32[12,8,128,128]{3,2,1,0:T(8,128)S(1)} %multiply_bitcast_fusion, s32[1,12]{1,0:T(1,128)S(1)} %copy-done.5), kind=kOutput, calls=%fused_computation.3 | convolution fusion | flops 18874380 | bytes 6815792 | tf_op jit(solution)/shard_map/b,bzxy->zxy/dot_general | solution.py:60
  384.9 0.8 broadcast_multiply_fusion
  385.8 1.7 constant_dynamic-slice_fusion.1
  387.5 3.2 constant_dynamic-slice_fusion
  390.8 4.9 fusion.40
  395.6 53.6 %reduce-scatter.2.cloned.1.call-done = f32[8,64,128]{2,1,0:T(8,128)} async-done(((f32[8,128,128]{2,1,0:T(8,128)}), f32[8,64,128]{2,1,0:T(8,128)}) %reduce-scatter.2.cloned.1.call-update) | async-done | bytes 262160 | tf_op jit(solution)/shard_map/reduce_scatter | solution.py:62
  449.3 1.1 fusion.47
  450.3 5.2 fusion.43
  455.6 39.6 %psum.15 = f32[8,9]{0,1:T(8,128)S(1)} all-reduce(f32[8,9]{0,1:T(8,128)S(1)} %pad_maximum_fusion.1), channel_id=1, replica_groups=mesh['ka'=2,'band'=16] {'ka','band'}, use_global_device_ids=true, to_apply=%region_2.3 | all-reduce | flops 72 | bytes 576 | tf_op jit(solution)/shard_map/psum | solution.py:69
  499.1 5.7 %fusion.34 = f32[1,8,64,128]{3,0,2,1:T(1,128)S(1)} fusion(f32[8,1,1,1]{0,1,3,2:T(1,128)S(1)} %convolution_bitcast_fusion, f32[8,8,64,128]{3,2,1,0:T(8,128)} %constant_dynamic-slice_fusion, f32[8,8,64,128]{3,2,1,0:T(8,128)S(1)} %constant_dynamic-slice_fusion.1), kind=kOutput, calls=%fused_computation.39 | convolution fusion | flops 7340032 | bytes 4456480 | tf_op jit(solution)/shard_map/h,hzxy->zxy/dot_general | solution.py:42
  504.9 8.4 %all_gather.7 = f32[8,128,128]{2,1,0:T(8,128)S(1)} all-gather(f32[8,64,128]{2,1,0:T(8,128)S(1)} %add_subtract_fusion), channel_id=1, replica_groups=mesh['ka'=2,'band'=16] {'ka'}, dimensions={1}, use_global_device_ids=true | all-gather | bytes 786432 | tf_op jit(solution)/shard_map/all_gather | solution.py:73
  513.3 7.3 %all_gather.6 = f32[8,128,128]{2,1,0:T(8,128)S(1)} all-gather(f32[8,64,128]{2,1,0:T(8,128)S(1)} %copy-done.3), channel_id=1, replica_groups=mesh['ka'=2,'band'=16] {'ka'}, dimensions={1}, use_global_device_ids=true | all-gather | bytes 786432 | tf_op jit(solution)/shard_map/all_gather | solution.py:72
  520.6 0.8 copy.125
  521.4 0.8 copy.126
  (31 shorter events, 4.1 us)
Async XLA Ops:
  7.2 8.3 %copy-start.1 = (f32[1,12,2,8,128,128]{5,4,3,2,1,0:T(8,128)S(1)}, f32[1,12,2,8,128,128]{5,4,3,2,1,0:T(8,128)}, u32[]{:S(2)}) copy-start(f32[1,12,2,8,128,128]{5,4,3,2,1,0:T(8,128)} %param.6) | copy-start | bytes 37748740
  53.5 8.2 %copy-start.2 = (f32[12,128,8,128]{3,1,2,0:T(8,128)S(1)}, f32[12,128,8,128]{3,1,2,0:T(8,128)}, u32[]{:S(2)}) copy-start(f32[12,128,8,128]{3,1,2,0:T(8,128)} %fusion.12) | copy-start | bytes 18874372
  94.8 231.1 %all-to-all-start = ((f32[12,2,128,8,128]{4,3,0,1,2:T(8,128)}), f32[12,2,128,8,128]{4,3,0,1,2:T(8,128)}, u32[]{:S(2)}, u32[]{:S(2)}) async-start(f32[12,2,128,8,128]{4,3,0,1,2:T(8,128)} %copy.60), calls=%async_computation | async-start | bytes 25165824 | tf_op jit(solution)/shard_map/all_to_all | solution.py:54
  102.2 347.0 %reduce-scatter.2.cloned.1.call-start = ((), (), s32[]{:S(2)}) async-start(), calls=%async_computation.2 | async-start | bytes 786432 | tf_op jit(solution)/shard_map/reduce_scatter | solution.py:62
  336.7 10.2 %copy-start = (f32[12,2,8,16,8,128]{5,4,3,2,1,0:T(8,128)S(1)}, f32[12,2,8,16,8,128]{5,4,3,2,1,0:T(8,128)}, u32[]{:S(2)}) copy-start(f32[12,2,8,16,8,128]{5,4,3,2,1,0:T(8,128)} %copy.121) | copy-start | bytes 37748740
  362.4 11.7 %copy-start.5 = (s32[1,12]{1,0:T(1,128)S(1)}, s32[1,12]{1,0:T(1,128)}, u32[]{:S(2)}) copy-start(s32[1,12]{1,0:T(1,128)} %param.7) | copy-start | bytes 148
  384.9 64.4 %copy-start.4 = (f32[8,128,128]{2,1,0:T(8,128)S(1)}, f32[8,128,128]{2,1,0:T(8,128)}, u32[]{:S(2)}) copy-start(f32[8,128,128]{2,1,0:T(8,128)} %param.9) | copy-start | bytes 1572868
  449.3 55.5 %copy-start.3 = (f32[8,64,128]{2,1,0:T(8,128)S(1)}, f32[8,64,128]{2,1,0:T(8,128)}, u32[]{:S(2)}) copy-start(f32[8,64,128]{2,1,0:T(8,128)} %reduce-scatter.2.cloned.1.call-done) | copy-start | bytes 786436
Sparse Core Ops, SparseCore 0:
  385.9 63.3 reduce-scatter.1
where the time goes:
time: 536 us; the launch traced here: 529 us
  waiting for transfers between devices  270 us (50%)
  matrix products  126 us (24%)
  blocking collectives  61.5 us (11%)
  local copies, waits for them, and re-layouts  34.6 us (6%)
  between operations  15.8 us (3%)
  other arithmetic  13.8 us (3%)
  starting transfers between devices  7.5 us (1%)
    all_to_all x1, waiting for transfers between devices, shards(): lax.all_to_all(stacked, 'band', split_axis=2, concat_axis=3, tiled=True)  216 us
    reduce_scatter x1, waiting for transfers between devices, shards(): share = lax.psum_scatter(pool_term, 'ka', scatter_dimension=1, tiled=True)  53.6 us
    psum x1, blocking collectives, shards(): summed = lax.psum(partial_terms, ('ka', 'band'))  39.6 us
    dot_general x3, matrix products, rotate(): einsum(pattern, imag_part, sine_table)  28 us
    dot_general x3, matrix products, rotate(): einsum(pattern, real_part, sine_table)  24.6 us
    dot_general x3, matrix products, rotate(): einsum(pattern, real_part, cosine_table)  23.6 us
    dot_general x3, matrix products, rotate(): einsum(pattern, imag_part, cosine_table)  23.4 us
    another operation x1, local copies, waits for them, and re-layouts, shards(): stacked = jnp.stack(after_ky, axis=1)  16.3 us
  transfers between devices with their start and end apart: 2, of which 2 were waited for; matrix products, arithmetic and copies ran while one was open for 2% of the time, Pallas kernels for 0%

commit v1 on v0

--- a/solution.py
+++ b/solution.py
@@ -66,7 +66,8 @@
     dens_part = lax.dynamic_slice_in_dim(dens_hist, share_start, share_width, 2)
     resid_part = lax.dynamic_slice_in_dim(resid_hist, share_start, share_width, 2)
     partial_terms = local_sums(share - base_density, resid_part)
-    summed = lax.psum(partial_terms, ("ka", "band"))
+    inner = lax.psum(partial_terms, "band")
+    summed = lax.psum(inner, "ka")
     mixed_share = finish_mix(share, base_density, dens_part, resid_part, summed)
     density, mixed_density = (
         lax.all_gather(share, "ka", axis=1, tiled=True),

time: 536 us -> 537 us (level)
    psum x1 -> x2, blocking collectives: 39.6 us -> 38.8 us  [the longest x1 33.5 us: shards(): inner = lax.psum(partial_terms, 'band')]
where the time goes in v1:
time: 537 us; the launch traced here: 530 us
  waiting for transfers between devices  270 us (50%)
  matrix products  126 us (23%)
  blocking collectives  61.7 us (11%)
  local copies, waits for them, and re-layouts  34.6 us (6%)
  between operations  15.8 us (3%)
  other arithmetic  13.8 us (3%)
  starting transfers between devices  7.5 us (1%)
    all_to_all x1, waiting for transfers between devices, shards(): lax.all_to_all(stacked, 'band', split_axis=2, concat_axis=3, tiled=True)  216 us
    reduce_scatter x1, waiting for transfers between devices, shards(): share = lax.psum_scatter(pool_term, 'ka', scatter_dimension=1, tiled=True)  53.6 us
    psum x1, blocking collectives, shards(): inner = lax.psum(partial_terms, 'band')  33.5 us
    dot_general x3, matrix products, rotate(): einsum(pattern, imag_part, sine_table)  28 us
    dot_general x3, matrix products, rotate(): einsum(pattern, real_part, sine_table)  24.6 us
    dot_general x3, matrix products, rotate(): einsum(pattern, real_part, cosine_table)  23.6 us
    dot_general x3, matrix products, rotate(): einsum(pattern, imag_part, cosine_table)  23.4 us
    another operation x1, local copies, waits for them, and re-layouts, shards(): stacked = jnp.stack(after_ky, axis=1)  16.3 us
  transfers between devices with their start and end apart: 2, of which 2 were waited for; matrix products, arithmetic and copies ran while one was open for 2% of the time, Pallas kernels for 0%

profile of v1, /device:TPU:0, one launch (start us, length us, event | category | flops | bytes accessed | tf_op | source)
XLA Modules:
  0.0 529.5 jit_solution(9208165874949613434)
XLA Ops:
  7.2 8.3 %fusion.2 = f32[128,12,8,128]{3,0,2,1:T(8,128)S(1)} fusion(f32[1,12,2,8,128,128]{5,4,3,2,1,0:T(8,128)} %param.6), kind=kOutput, calls=%fused_computation.7 | convolution fusion | flops 2416148480 | bytes 12582912 | tf_op jit(solution)/shard_map/bpqk,kz->bzpq/dot_general | solution.py:23
  15.5 6.2 %fusion.6 = f32[128,12,8,128]{3,0,2,1:T(8,128)S(1)} fusion(f32[1,12,2,8,128,128]{5,4,3,2,1,0:T(8,128)S(1)} %copy-done.1), kind=kOutput, calls=%fused_computation.11 | convolution fusion | flops 2416148480 | bytes 12582912 | tf_op jit(solution)/shard_map/bpqk,kz->bzpq/dot_general | solution.py:23
  21.7 8.7 %fusion.4 = f32[128,12,8,128]{3,0,2,1:T(8,128)S(1)} fusion(f32[1,12,2,8,128,128]{5,4,3,2,1,0:T(8,128)} %param.6), kind=kOutput, calls=%fused_computation.9 | convolution fusion | flops 2416148480 | bytes 12582912 | tf_op jit(solution)/shard_map/bpqk,kz->bzpq/dot_general | solution.py:22
  30.3 8.1 %fusion.8 = f32[128,12,8,128]{3,0,2,1:T(8,128)S(1)} fusion(f32[1,12,2,8,128,128]{5,4,3,2,1,0:T(8,128)} %param.6), kind=kOutput, calls=%fused_computation.13 | convolution fusion | flops 2416148480 | bytes 12582912 | tf_op jit(solution)/shard_map/bpqk,kz->bzpq/dot_general | solution.py:22
  38.5 7.4 %fusion.10 = f32[12,128,8,128]{3,1,2,0:T(8,128)} fusion(f32[128,12,8,128]{3,0,2,1:T(8,128)S(1)} %fusion.6, f32[128,12,8,128]{3,0,2,1:T(8,128)S(1)} %fusion.2), kind=kOutput, calls=%fused_computation.15 | convolution fusion | flops 2417721344 | bytes 18874368 | tf_op jit(solution)/shard_map/bzpq,qy->bzpy/dot_general | solution.py:23
  45.8 7.7 %fusion.12 = f32[12,128,8,128]{3,1,2,0:T(8,128)} fusion(f32[128,12,8,128]{3,0,2,1:T(8,128)S(1)} %fusion.6, f32[128,12,8,128]{3,0,2,1:T(8,128)S(1)} %fusion.2), kind=kOutput, calls=%fused_computation.17 | convolution fusion | flops 2417721344 | bytes 18874368 | tf_op jit(solution)/shard_map/bzpq,qy->bzpy/dot_general | solution.py:22
  53.5 8.2 %add_bitcast_fusion = f32[12,1,128,8,128]{4,2,3,0,1:T(8,128)S(1)} fusion(f32[12,128,8,128]{3,1,2,0:T(8,128)} %fusion.10, f32[128,12,8,128]{3,0,2,1:T(8,128)S(1)} %fusion.8, f32[128,12,8,128]{3,0,2,1:T(8,128)S(1)} %fusion.4), kind=kOutput, calls=%fused_computation.24 | convolution fusion | flops 2419294208 | bytes 25165824 | tf_op jit(solution)/shard_map/bzpq,qy->bzpy/dot_general | solution.py:23
  61.7 7.7 %subtract_bitcast_fusion = f32[12,1,128,8,128]{4,2,3,0,1:T(8,128)} fusion(f32[12,128,8,128]{3,1,2,0:T(8,128)S(1)} %copy-done.2, f32[128,12,8,128]{3,0,2,1:T(8,128)S(1)} %fusion.8, f32[128,12,8,128]{3,0,2,1:T(8,128)S(1)} %fusion.4), kind=kOutput, calls=%fused_computation.25 | convolution fusion | flops 2419294208 | bytes 25165824 | tf_op jit(solution)/shard_map/bzpq,qy->bzpy/dot_general | solution.py:22
  69.4 9.0 %pad_maximum_fusion = f32[12,2,128,8,128]{4,2,3,0,1:T(8,128)} fusion(f32[12,1,128,8,128]{4,2,3,0,1:T(8,128)S(1)} %add_bitcast_fusion, f32[12,1,128,8,128]{4,2,3,0,1:T(8,128)} %subtract_bitcast_fusion), kind=kLoop, calls=%fused_computation.1 | loop fusion | flops 3145728 | bytes 25165824 | tf_op jit(solution)/shard_map/stack | solution.py:53
  78.4 16.3 %copy.60 = f32[12,2,128,8,128]{4,3,0,1,2:T(8,128)} copy(f32[12,2,128,8,128]{4,2,3,0,1:T(8,128)} %pad_maximum_fusion) | data formatting | bytes 25165824 | tf_op jit(solution)/shard_map/stack | solution.py:53
  94.8 7.5 %all-to-all-start = ((f32[12,2,128,8,128]{4,3,0,1,2:T(8,128)}), f32[12,2,128,8,128]{4,3,0,1,2:T(8,128)}, u32[]{:S(2)}, u32[]{:S(2)}) async-start(f32[12,2,128,8,128]{4,3,0,1,2:T(8,128)} %copy.60), calls=%async_computation | async-start | bytes 25165824 | tf_op jit(solution)/shard_map/all_to_all | solution.py:54
  102.9 6.1 %psum.21 = f32[]{:T(128)} all-reduce(f32[]{:T(128)} %bitcast.28), channel_id=1, replica_groups=mesh['ka'=2,'band'=16] {'ka'}, use_global_device_ids=true, to_apply=%region_0.1 | all-reduce | flops 1 | bytes 8 | tf_op jit(solution)/shard_map/psum | solution.py:50
  109.7 216.1 %all-to-all-done = f32[12,2,128,8,128]{4,3,0,1,2:T(8,128)} async-done(((f32[12,2,128,8,128]{4,3,0,1,2:T(8,128)}), f32[12,2,128,8,128]{4,3,0,1,2:T(8,128)}, u32[]{:S(2)}, u32[]{:S(2)}) %all-to-all-start) | async-done | bytes 12582944 | tf_op jit(solution)/shard_map/all_to_all | solution.py:54
  325.8 10.8 %copy.121 = f32[12,2,8,16,8,128]{5,4,3,2,1,0:T(8,128)} copy(f32[12,2,8,16,8,128]{5,4,0,1,2,3:T(8,128)} %bitcast.18) | data formatting | bytes 25165824 | tf_op jit(solution)/shard_map/all_to_all | solution.py:54
  336.7 10.2 %fusion.18 = f32[128,12,8,128]{3,0,2,1:T(8,128)} fusion(f32[12,2,8,128,128]{4,3,2,1,0:T(8,128)} %bitcast.136), kind=kOutput, calls=%fused_computation.26 | convolution fusion | flops 2416148480 | bytes 12582912 | tf_op jit(solution)/shard_map/bzpy,px->bzxy/dot_general | solution.py:23
  346.9 7.8 %fusion.19 = f32[128,12,8,128]{3,0,2,1:T(8,128)} fusion(f32[12,2,8,128,128]{4,3,2,1,0:T(8,128)S(1)} %bitcast.137), kind=kOutput, calls=%fused_computation.27 | convolution fusion | flops 2416148480 | bytes 12582912 | tf_op jit(solution)/shard_map/bzpy,px->bzxy/dot_general | solution.py:22
  354.7 7.8 %fusion.20 = f32[128,12,8,128]{3,0,2,1:T(8,128)} fusion(f32[12,2,8,128,128]{4,3,2,1,0:T(8,128)S(1)} %bitcast.138), kind=kOutput, calls=%fused_computation.28 | convolution fusion | flops 2416148480 | bytes 12582912 | tf_op jit(solution)/shard_map/bzpy,px->bzxy/dot_general | solution.py:23
  362.4 11.7 %multiply_bitcast_fusion = f32[12,8,128,128]{3,2,1,0:T(8,128)S(1)} fusion(f32[128,12,8,128]{3,0,2,1:T(8,128)} %fusion.18, f32[128,12,8,128]{3,0,2,1:T(8,128)} %fusion.20, f32[128,12,8,128]{3,0,2,1:T(8,128)} %fusion.19, f32[12,2,8,128,128]{4,3,2,1,0:T(8,128)S(1)} %bitcast.139), kind=kOutput, calls=%fused_computation.23 | convolution fusion | flops 2425585664 | bytes 31457280 | tf_op jit(solution)/shard_map/bzpy,px->bzxy/dot_general | solution.py:22
  374.1 10.8 %fusion = f32[1,8,128,128]{3,0,2,1:T(1,128)S(1)} fusion(f32[12,8,128,128]{3,2,1,0:T(8,128)S(1)} %multiply_bitcast_fusion, s32[1,12]{1,0:T(1,128)S(1)} %copy-done.5), kind=kOutput, calls=%fused_computation.3 | convolution fusion | flops 18874380 | bytes 6815792 | tf_op jit(solution)/shard_map/b,bzxy->zxy/dot_general | solution.py:60
  384.9 0.8 broadcast_multiply_fusion
  385.8 1.7 constant_dynamic-slice_fusion.1
  387.5 3.2 constant_dynamic-slice_fusion
  390.8 4.9 fusion.40
  395.6 53.6 %reduce-scatter.2.cloned.1.call-done = f32[8,64,128]{2,1,0:T(8,128)} async-done(((f32[8,128,128]{2,1,0:T(8,128)}), f32[8,64,128]{2,1,0:T(8,128)}) %reduce-scatter.2.cloned.1.call-update) | async-done | bytes 262160 | tf_op jit(solution)/shard_map/reduce_scatter | solution.py:62
  449.3 1.1 fusion.47
  450.3 5.2 fusion.43
  455.6 33.5 %psum.22 = f32[8,9]{0,1:T(8,128)S(1)} all-reduce(f32[8,9]{0,1:T(8,128)S(1)} %pad_maximum_fusion.1), channel_id=1, replica_groups=mesh['ka'=2,'band'=16] {'band'}, use_global_device_ids=true, to_apply=%region_2.3 | all-reduce | flops 72 | bytes 576 | tf_op jit(solution)/shard_map/psum | solution.py:69
  489.1 5.2 psum.23
  498.3 5.7 %fusion.34 = f32[1,8,64,128]{3,0,2,1:T(1,128)S(1)} fusion(f32[8,1,1,1]{0,1,3,2:T(1,128)S(1)} %convolution_bitcast_fusion, f32[8,8,64,128]{3,2,1,0:T(8,128)} %constant_dynamic-slice_fusion, f32[8,8,64,128]{3,2,1,0:T(8,128)S(1)} %constant_dynamic-slice_fusion.1), kind=kOutput, calls=%fused_computation.39 | convolution fusion | flops 7340032 | bytes 4456480 | tf_op jit(solution)/shard_map/h,hzxy->zxy/dot_general | solution.py:42
  504.0 9.8 %all_gather.7 = f32[8,128,128]{2,1,0:T(8,128)S(1)} all-gather(f32[8,64,128]{2,1,0:T(8,128)S(1)} %add_subtract_fusion), channel_id=1, replica_groups=mesh['ka'=2,'band'=16] {'ka'}, dimensions={1}, use_global_device_ids=true | all-gather | bytes 786432 | tf_op jit(solution)/shard_map/all_gather | solution.py:74
  513.8 7.0 %all_gather.6 = f32[8,128,128]{2,1,0:T(8,128)S(1)} all-gather(f32[8,64,128]{2,1,0:T(8,128)S(1)} %copy-done.3), channel_id=1, replica_groups=mesh['ka'=2,'band'=16] {'ka'}, dimensions={1}, use_global_device_ids=true | all-gather | bytes 786432 | tf_op jit(solution)/shard_map/all_gather | solution.py:73
  520.8 0.8 copy.125
  (32 shorter events, 4.9 us)
Async XLA Ops:
  7.2 8.3 %copy-start.1 = (f32[1,12,2,8,128,128]{5,4,3,2,1,0:T(8,128)S(1)}, f32[1,12,2,8,128,128]{5,4,3,2,1,0:T(8,128)}, u32[]{:S(2)}) copy-start(f32[1,12,2,8,128,128]{5,4,3,2,1,0:T(8,128)} %param.6) | copy-start | bytes 37748740
  53.5 8.2 %copy-start.2 = (f32[12,128,8,128]{3,1,2,0:T(8,128)S(1)}, f32[12,128,8,128]{3,1,2,0:T(8,128)}, u32[]{:S(2)}) copy-start(f32[12,128,8,128]{3,1,2,0:T(8,128)} %fusion.12) | copy-start | bytes 18874372
  94.8 231.1 %all-to-all-start = ((f32[12,2,128,8,128]{4,3,0,1,2:T(8,128)}), f32[12,2,128,8,128]{4,3,0,1,2:T(8,128)}, u32[]{:S(2)}, u32[]{:S(2)}) async-start(f32[12,2,128,8,128]{4,3,0,1,2:T(8,128)} %copy.60), calls=%async_computation | async-start | bytes 25165824 | tf_op jit(solution)/shard_map/all_to_all | solution.py:54
  102.2 347.0 %reduce-scatter.2.cloned.1.call-start = ((), (), s32[]{:S(2)}) async-start(), calls=%async_computation.2 | async-start | bytes 786432 | tf_op jit(solution)/shard_map/reduce_scatter | solution.py:62
  336.7 10.2 %copy-start = (f32[12,2,8,16,8,128]{5,4,3,2,1,0:T(8,128)S(1)}, f32[12,2,8,16,8,128]{5,4,3,2,1,0:T(8,128)}, u32[]{:S(2)}) copy-start(f32[12,2,8,16,8,128]{5,4,3,2,1,0:T(8,128)} %copy.121) | copy-start | bytes 37748740
  362.4 11.7 %copy-start.5 = (s32[1,12]{1,0:T(1,128)S(1)}, s32[1,12]{1,0:T(1,128)}, u32[]{:S(2)}) copy-start(s32[1,12]{1,0:T(1,128)} %param.7) | copy-start | bytes 148
  384.9 64.4 %copy-start.4 = (f32[8,128,128]{2,1,0:T(8,128)S(1)}, f32[8,128,128]{2,1,0:T(8,128)}, u32[]{:S(2)}) copy-start(f32[8,128,128]{2,1,0:T(8,128)} %param.9) | copy-start | bytes 1572868
  449.3 54.7 %copy-start.3 = (f32[8,64,128]{2,1,0:T(8,128)S(1)}, f32[8,64,128]{2,1,0:T(8,128)}, u32[]{:S(2)}) copy-start(f32[8,64,128]{2,1,0:T(8,128)} %reduce-scatter.2.cloned.1.call-done) | copy-start | bytes 786436
Sparse Core Ops, SparseCore 0:
  385.9 63.3 reduce-scatter.1
